TPU v7x, 8 devices: a whole 2x2x1 slice. The times are simulated.
8 devices in a mesh: col: 2 (over z, y), row: 4 (over x, core).
Axes of the slice: x: 2, y: 2, z: 1, core: 2. Of those that a mesh axis runs over, the one named last changes fastest.
Arguments:
- adjacency: bfloat16 [16384, 16384], P('row', 'col')
- pers_vec: float32 [16384, 128], P(('row', 'col'))
- restart_wt: float32 [32, 128], replicated
Outputs:
- output 1: float32 [16384, 128], P(('col', 'row'))
- output 2: float32 [16384, 128], P(('row', 'col'))
All inputs are finite; a program needn't handle non-finite values.
Results may differ from a plain program's by a relative error of at most 0.001.
Values are sent between devices in bfloat16 or wider.
A program may use at most 1 GiB of HBM per device.

v0:
```python
import jax
import jax.numpy as jnp
from jax import lax
from jax.sharding import PartitionSpec as P


def col_normalise(local_vals, n_total):
    sq_sum = lax.psum(jnp.sum(local_vals * local_vals, axis=0, keepdims=True), ("col", "row"))
    return local_vals * lax.rsqrt(sq_sum / n_total)


def solution(mesh):
    row_size = mesh.shape["row"]

    def device_fn(adj_tile, pers_piece, restart_wt):
        n_total = adj_tile.shape[0] * row_size
        hub_vec = pers_piece
        for sweep_idx in range(restart_wt.shape[0]):
            weight = restart_wt[sweep_idx]
            hub_block = lax.all_gather(hub_vec.astype(jnp.bfloat16), "col", axis=0, tiled=True)
            auth_part = lax.dot_general(adj_tile, hub_block, (((0,), (0,)), ((), ())), preferred_element_type=jnp.float32)
            auth_sum = lax.psum_scatter(auth_part, "row", scatter_dimension=0, tiled=True)
            auth_vec = col_normalise(auth_sum, n_total)
            auth_block = lax.all_gather(auth_vec.astype(jnp.bfloat16), "row", axis=0, tiled=True)
            hub_part = jnp.dot(adj_tile, auth_block, preferred_element_type=jnp.float32)
            hub_sum = lax.psum_scatter(hub_part, "col", scatter_dimension=0, tiled=True)
            hub_vec = (1.0 - weight) * col_normalise(hub_sum, n_total) + weight * pers_piece
        return auth_vec, hub_vec

    return jax.shard_map(device_fn, mesh=mesh, in_specs=(P("row", "col"), P(("row", "col"), None), P(None, None)), out_specs=(P(("col", "row"), None), P(("row", "col"), None)), check_vma=False)
```

profile of v0, /device:TPU:0, one launch (start us, length us, event | category | flops | bytes accessed | tf_op | source)
XLA Modules:
  0.0 6945.7 jit_solution(18269030844405517695)
XLA Ops:
  60.1 38.4 reduce-scatter.65.cloned.1.call-done
  276.9 38.4 reduce-scatter.69.cloned.1.call-done
  709.6 38.4 reduce-scatter.77.cloned.1.call-done
  926.0 38.4 reduce-scatter.81.cloned.1.call-done
  1142.3 38.4 reduce-scatter.85.cloned.1.call-done
  1358.7 38.4 reduce-scatter.89.cloned.1.call-done
  1575.0 38.4 reduce-scatter.93.cloned.1.call-done
  2007.7 38.4 reduce-scatter.101.cloned.1.call-done
  2440.5 38.4 reduce-scatter.109.cloned.1.call-done
  2656.8 38.4 reduce-scatter.113.cloned.1.call-done
  2873.2 38.4 reduce-scatter.117.cloned.1.call-done
  4171.3 38.4 reduce-scatter.141.cloned.1.call-done
  4387.6 38.4 reduce-scatter.145.cloned.1.call-done
  4604.0 38.4 reduce-scatter.149.cloned.1.call-done
  4820.4 38.4 reduce-scatter.153.cloned.1.call-done
  5036.7 38.4 reduce-scatter.157.cloned.1.call-done
  5253.1 38.4 reduce-scatter.161.cloned.1.call-done
  5469.5 38.4 reduce-scatter.165.cloned.1.call-done
  5685.8 38.4 reduce-scatter.169.cloned.1.call-done
  5902.2 38.4 reduce-scatter.173.cloned.1.call-done
  6118.5 38.4 reduce-scatter.177.cloned.1.call-done
  6334.9 38.4 reduce-scatter.181.cloned.1.call-done
  6551.3 38.4 reduce-scatter.185.cloned.1.call-done
  6767.6 38.4 reduce-scatter.189.cloned.1.call-done
  (792 shorter events, 6006.8 us)
Async XLA Ops:
  9.3 89.2 %reduce-scatter.65.cloned.1.call-start = ((), (), s32[]{:S(2)}) async-start(), calls=%async_computation.65 | async-start | bytes 5242880 | tf_op jit(solution)/shard_map/reduce_scatter | solution.py:22
  60.1 85.7 %all-gather.67.cloned.1.call-start = ((), (), s32[]{:S(2)}) async-start(), calls=%async_computation.66 | async-start | bytes 2621440 | tf_op jit(solution)/shard_map/all_gather | solution.py:24
  493.2 85.6 %all-gather.75.cloned.1.call-start = ((), (), s32[]{:S(2)}) async-start(), calls=%async_computation.74 | async-start | bytes 2621440 | tf_op jit(solution)/shard_map/all_gather | solution.py:24
  709.5 85.6 %all-gather.79.cloned.1.call-start = ((), (), s32[]{:S(2)}) async-start(), calls=%async_computation.78 | async-start | bytes 2621440 | tf_op jit(solution)/shard_map/all_gather | solution.py:24
  925.9 85.6 %all-gather.83.cloned.1.call-start = ((), (), s32[]{:S(2)}) async-start(), calls=%async_computation.82 | async-start | bytes 2621440 | tf_op jit(solution)/shard_map/all_gather | solution.py:24
  1142.3 85.6 %all-gather.87.cloned.1.call-start = ((), (), s32[]{:S(2)}) async-start(), calls=%async_computation.86 | async-start | bytes 2621440 | tf_op jit(solution)/shard_map/all_gather | solution.py:24
  1358.6 85.6 %all-gather.91.cloned.1.call-start = ((), (), s32[]{:S(2)}) async-start(), calls=%async_computation.90 | async-start | bytes 2621440 | tf_op jit(solution)/shard_map/all_gather | solution.py:24
  2007.7 85.6 %all-gather.103.cloned.1.call-start = ((), (), s32[]{:S(2)}) async-start(), calls=%async_computation.102 | async-start | bytes 2621440 | tf_op jit(solution)/shard_map/all_gather | solution.py:24
  2440.4 85.6 %all-gather.111.cloned.1.call-start = ((), (), s32[]{:S(2)}) async-start(), calls=%async_computation.110 | async-start | bytes 2621440 | tf_op jit(solution)/shard_map/all_gather | solution.py:24
  2656.8 85.6 %all-gather.115.cloned.1.call-start = ((), (), s32[]{:S(2)}) async-start(), calls=%async_computation.114 | async-start | bytes 2621440 | tf_op jit(solution)/shard_map/all_gather | solution.py:24
  2873.1 85.6 %all-gather.119.cloned.1.call-start = ((), (), s32[]{:S(2)}) async-start(), calls=%async_computation.118 | async-start | bytes 2621440 | tf_op jit(solution)/shard_map/all_gather | solution.py:24
  4171.2 85.6 %all-gather.143.cloned.1.call-start = ((), (), s32[]{:S(2)}) async-start(), calls=%async_computation.142 | async-start | bytes 2621440 | tf_op jit(solution)/shard_map/all_gather | solution.py:24
  4387.6 85.6 %all-gather.147.cloned.1.call-start = ((), (), s32[]{:S(2)}) async-start(), calls=%async_computation.146 | async-start | bytes 2621440 | tf_op jit(solution)/shard_map/all_gather | solution.py:24
  4604.0 85.6 %all-gather.151.cloned.1.call-start = ((), (), s32[]{:S(2)}) async-start(), calls=%async_computation.150 | async-start | bytes 2621440 | tf_op jit(solution)/shard_map/all_gather | solution.py:24
  4820.3 85.6 %all-gather.155.cloned.1.call-start = ((), (), s32[]{:S(2)}) async-start(), calls=%async_computation.154 | async-start | bytes 2621440 | tf_op jit(solution)/shard_map/all_gather | solution.py:24
  5036.7 85.6 %all-gather.159.cloned.1.call-start = ((), (), s32[]{:S(2)}) async-start(), calls=%async_computation.158 | async-start | bytes 2621440 | tf_op jit(solution)/shard_map/all_gather | solution.py:24
  5253.0 85.6 %all-gather.163.cloned.1.call-start = ((), (), s32[]{:S(2)}) async-start(), calls=%async_computation.162 | async-start | bytes 2621440 | tf_op jit(solution)/shard_map/all_gather | solution.py:24
  5469.4 85.6 %all-gather.167.cloned.1.call-start = ((), (), s32[]{:S(2)}) async-start(), calls=%async_computation.166 | async-start | bytes 2621440 | tf_op jit(solution)/shard_map/all_gather | solution.py:24
  5685.8 85.6 %all-gather.171.cloned.1.call-start = ((), (), s32[]{:S(2)}) async-start(), calls=%async_computation.170 | async-start | bytes 2621440 | tf_op jit(solution)/shard_map/all_gather | solution.py:24
  5902.1 85.6 %all-gather.175.cloned.1.call-start = ((), (), s32[]{:S(2)}) async-start(), calls=%async_computation.174 | async-start | bytes 2621440 | tf_op jit(solution)/shard_map/all_gather | solution.py:24
  6118.5 85.6 %all-gather.179.cloned.1.call-start = ((), (), s32[]{:S(2)}) async-start(), calls=%async_computation.178 | async-start | bytes 2621440 | tf_op jit(solution)/shard_map/all_gather | solution.py:24
  6334.9 85.6 %all-gather.183.cloned.1.call-start = ((), (), s32[]{:S(2)}) async-start(), calls=%async_computation.182 | async-start | bytes 2621440 | tf_op jit(solution)/shard_map/all_gather | solution.py:24
  6551.2 85.6 %all-gather.187.cloned.1.call-start = ((), (), s32[]{:S(2)}) async-start(), calls=%async_computation.186 | async-start | bytes 2621440 | tf_op jit(solution)/shard_map/all_gather | solution.py:24
  6767.6 85.7 %all-gather.191.cloned.1.call-start = ((), (), s32[]{:S(2)}) async-start(), calls=%async_computation.190 | async-start | bytes 2621440 | tf_op jit(solution)/shard_map/all_gather | solution.py:24
  (156 other events, 13341.7 us)
Sparse Core Ops, SparseCore 0:
  60.2 38.2 reduce-scatter.64
  277.0 38.2 reduce-scatter.68
  493.3 38.2 reduce-scatter.72
  709.7 38.2 reduce-scatter.76
  1142.4 38.2 reduce-scatter.84
  1358.8 38.2 reduce-scatter.88
  1575.1 38.2 reduce-scatter.92
  2007.8 38.2 reduce-scatter.100
  2440.5 38.2 reduce-scatter.108
  2656.9 38.2 reduce-scatter.112
  2873.3 38.2 reduce-scatter.116
  4171.4 38.2 reduce-scatter.140
  4387.7 38.2 reduce-scatter.144
  4604.1 38.2 reduce-scatter.148
  4820.4 38.2 reduce-scatter.152
  5036.8 38.2 reduce-scatter.156
  5253.2 38.2 reduce-scatter.160
  5469.5 38.2 reduce-scatter.164
  5685.9 38.2 reduce-scatter.168
  5902.2 38.2 reduce-scatter.172
  6118.6 38.2 reduce-scatter.176
  6335.0 38.2 reduce-scatter.180
  6551.3 38.2 reduce-scatter.184
  6767.7 38.2 reduce-scatter.188
  (104 shorter events, 2548.4 us)
where the time goes:
time: 6970 us; the launch traced here: 6950 us
  waiting for transfers between devices  3480 us (50%)
  matrix products  1780 us (26%)
  blocking collectives  1420 us (20%)
  other arithmetic  233 us (3%)
    psum x64, blocking collectives, col_normalise(): lax.psum(jnp.sum(local_vals * local_vals, axis=0, keepdims=True), ('col',...  1420 us
    reduce_scatter x32, waiting for transfers between devices, device_fn(): lax.psum_scatter(auth_part, 'row', scatter_dimension=0, tiled=True)  1230 us
    dot_general x32, matrix products, device_fn(): hub_part = jnp.dot(adj_tile, auth_block, preferred_element_type=jnp.float32)  945 us
    reduce_scatter x32, waiting for transfers between devices, device_fn(): hub_sum = lax.psum_scatter(hub_part, 'col', scatter_dimension=0, tiled=True)  928 us
    dot_general x32, matrix products, device_fn(): lax.dot_general(adj_tile, hub_block, (((0,), (0,)), ((), ())), preferred_...  832 us
    all_gather x32, waiting for transfers between devices, device_fn(): lax.all_gather(auth_vec.astype(jnp.bfloat16), 'row', axis=0, tiled=True)  680 us
    all_gather x32, waiting for transfers between devices, device_fn(): lax.all_gather(hub_vec.astype(jnp.bfloat16), 'col', axis=0, tiled=True)  642 us
  transfers between devices with their start and end apart: 128, of which 128 were waited for; matrix products, arithmetic and copies ran while one was open for 0% of the time, Pallas kernels for 0%

commit v1 on v0

v1 whole, which is shorter than its diff:
```python
import jax
import jax.numpy as jnp
from jax import lax
from jax.experimental import pallas as pl
from jax.experimental.pallas import tpu as pltpu
from jax.sharding import PartitionSpec as P

MESH = pl.DeviceIdType.MESH
F32 = jnp.float32
BF16 = jnp.bfloat16
GROUPS = 2
RING = 3


def dot_plain(lhs, rhs):
    return lax.dot_general(lhs, rhs, (((1,), (0,)), ((), ())), preferred_element_type=F32)


def dot_trans(lhs, rhs):
    return lax.dot_general(lhs, rhs, (((1,), (1,)), ((), ())), preferred_element_type=F32)


def make_kernel(sweeps, n_total, piece, half_len, m):
    n_blocks = sweeps * 32
    step_len = 512
    n_steps = piece // step_len
    steps_half = half_len // step_len

    def kernel(adj, adj_t, start, weights, auth_out, hub_out, res, ring, part, pair_recv, recv, auth, hub, norm_send, norm_recv,
               res_sem, ring_sem, pair_ss, pair_rs, link_ss, link_rs, norm_ss, norm_rs, auth_ss, auth_rs, hub_ss, hub_rs):
        j = lax.axis_index("col")
        i = lax.axis_index("row")
        x = i // 2
        c = i % 2
        own_row = pl.multiple_of(j * piece, piece)
        far_row = pl.multiple_of((1 - j) * piece, piece)
        pair_dev = (j, 2 * x + 1 - c)
        x_dev = (j, 2 * (1 - x) + c)
        y_dev = (1 - j, i)

        def piece_of(px, pc):
            return pl.ds(pl.multiple_of((2 * px + pc) * piece, piece), piece)

        own_cols = piece_of(x, c)
        pair_cols = piece_of(x, 1 - c)
        far_cols = piece_of(1 - x, c)
        far_pair_cols = piece_of(1 - x, 1 - c)

        def relative(r):
            rj, rx, rc = r // 4, (r // 2) % 2, r % 2
            jj = 1 - j if rj else j
            xx = 1 - x if rx else x
            cc = 1 - c if rc else c
            return (jj, 2 * xx + cc)

        def remote(src, dst, ss, rs, dev):
            return pltpu.make_async_remote_copy(src_ref=src, dst_ref=dst, send_sem=ss, recv_sem=rs, device_id=dev, device_id_type=MESH)

        def pair_copy(g, slot, half):
            return remote(part.at[g, 2 * slot, half], pair_recv.at[g, slot, half], pair_ss.at[g, slot, half], pair_rs.at[g, slot, half], pair_dev)

        def x_copy(g, half):
            return remote(part.at[g, 1, half], recv.at[g, half], link_ss.at[0, g, half], link_rs.at[0, g, half], x_dev)

        def y_copy(g, half):
            return remote(part.at[g, 0, half], recv.at[g, half], link_ss.at[1, g, half], link_rs.at[1, g, half], y_dev)

        def norm_copy(phase, g, r):
            return remote(norm_send.at[phase, g], norm_recv.at[phase, g, r - 1], norm_ss.at[phase, g, r - 1], norm_rs.at[phase, g, r - 1], relative(r))

        def auth_pair(g):
            return remote(auth.at[g, :, own_cols], auth.at[g, :, own_cols], auth_ss.at[g, 0], auth_rs.at[g, 0], pair_dev)

        def auth_x(g):
            return remote(auth.at[g, :, own_cols], auth.at[g, :, own_cols], auth_ss.at[g, 1], auth_rs.at[g, 1], x_dev)

        def auth_forward(g):
            return remote(auth.at[g, :, far_cols], auth.at[g, :, far_cols], auth_ss.at[g, 2], auth_rs.at[g, 2], pair_dev)

        def hub_y(g):
            return remote(hub.at[g, 0], hub.at[g, 1], hub_ss.at[g], hub_rs.at[g], y_dev)

        def block_copy(t, first):
            buf = t % RING
            b = t % 8
            if first:
                o = b // 2
                cols = (2 * ((x + 1 - o // 2) % 2) + (c + 1 + o) % 2) * piece + (b % 2) * half_len
                src = adj.at[pl.ds(far_row, piece), pl.ds(pl.multiple_of(cols, half_len), half_len)]
            else:
                kp = b % 4
                rows = (2 * ((x + kp // 2) % 2) + (c + kp) % 2) * piece
                cols = (b // 4) * half_len
                src = adj_t.at[pl.ds(pl.multiple_of(rows, piece), piece), pl.ds(pl.multiple_of(cols, half_len), half_len)]
            return pltpu.make_async_copy(src, ring.at[buf], ring_sem.at[buf])

        def block_start(t):
            first = (t // 8) % 4 < 2

            @pl.when(jnp.logical_and(t < n_blocks, first))
            def _():
                block_copy(t, True).start()

            @pl.when(jnp.logical_and(t < n_blocks, jnp.logical_not(first)))
            def _():
                block_copy(t, False).start()

        def sum_squares(vals):
            sq = None
            for val in vals:
                val = val * val
                for q in range(half_len // 128):
                    cur = val[:, q * 128:(q + 1) * 128]
                    sq = cur if sq is None else sq + cur
            padded = jnp.concatenate([sq, jnp.zeros((128 - m, 128), F32)], axis=0)
            return jnp.sum(padded.T, axis=0, keepdims=True)

        def spread(row):
            return jnp.broadcast_to(row, (128, 128)).T

        def norm_start(phase, g, vals):
            norm_send[phase, g] = jnp.broadcast_to(sum_squares(vals), (8, 128))
            for r in range(1, 8):
                norm_copy(phase, g, r).start()

        def norm_finish(phase, g):
            total = norm_send[phase, g]
            for r in range(1, 8):
                norm_copy(phase, g, r).wait_recv()
                total = total + norm_recv[phase, g, r - 1]
            for r in range(1, 8):
                norm_copy(phase, g, r).wait_send()
            return spread(lax.rsqrt(total[0:1, :] / n_total))[:m, 0:1]

        def auth_sum(g):
            vals = []
            for half in range(2):
                pair_copy(g, 1, half).wait_recv()
                x_copy(g, half).wait_recv()
                val = part[g, 3, half] + pair_recv[g, 1, half] + recv[g, half]
                part[g, 3, half] = val
                vals.append(val)
            norm_start(0, g, vals)

        def auth_finish(g):
            scale = norm_finish(0, g)
            for half in range(2):
                val = part[g, 3, half] * scale
                cols = pl.ds(half * half_len, half_len)
                auth_out[g, :, cols] = val
                base = pl.multiple_of((2 * x + c) * piece + half * half_len, half_len)
                auth[g, :, pl.ds(base, half_len)] = val.astype(BF16)
            auth_x(g).start()
            auth_pair(g).start()
            for half in range(2):
                pair_copy(g, 0, half).wait_send()
                pair_copy(g, 1, half).wait_send()
                x_copy(g, half).wait_send()

        def hub_sum(g):
            vals = []
            for half in range(2):
                y_copy(g, half).wait_recv()
                val = part[g, 3, half] + recv[g, half]
                part[g, 3, half] = val
                vals.append(val)
            norm_start(1, g, vals)

        def hub_finish(g, k, send):
            scale = norm_finish(1, g)
            row = weights[g, pl.ds(k, 1), :]
            weight = spread(row)[:m, 0:1]
            for half in range(2):
                cols = pl.ds(half * half_len, half_len)
                val = (1.0 - weight) * (part[g, 3, half] * scale) + weight * start[g, :, cols]
                hub_out[g, :, cols] = val
                hub[g, 0, :, cols] = val.astype(BF16)

            if send is not None:
                @pl.when(send)
                def _():
                    hub_y(g).start()

            for half in range(2):
                y_copy(g, half).wait_send()
            auth_pair(g).wait_send()
            auth_x(g).wait_send()
            auth_forward(g).wait_send()

        barrier = pltpu.get_barrier_semaphore()
        for r in range(1, 8):
            pl.semaphore_signal(barrier, inc=1, device_id=relative(r), device_id_type=MESH)
        pl.semaphore_wait(barrier, 7)

        res_copy = pltpu.make_async_copy(adj.at[pl.ds(own_row, piece), :], res, res_sem)
        res_copy.start()
        for t in range(RING):
            block_copy(t, True).start()
        for g in range(GROUPS):
            hub[g, 0] = start[g].astype(BF16)
            hub_y(g).start()
        res_copy.wait()

        def sweep(k, carry):
            base = k * 32

            def first_product(g, carry):
                def chunk(b, carry):
                    t = base + g * 8 + b
                    o, half = b // 2, b % 2
                    cols = (2 * ((x + 1 - o // 2) % 2) + (c + 1 + o) % 2) * piece + half * half_len

                    @pl.when(b == 0)
                    def _():
                        hub_y(g).wait()

                    block_copy(t, True).wait()
                    acc = dot_plain(hub[g, 1], ring[t % RING])
                    acc = acc + dot_plain(hub[g, 0], res[:, pl.ds(pl.multiple_of(cols, half_len), half_len)])
                    part[g, o, half] = acc
                    block_start(t + RING)

                    @pl.when(o == 0)
                    def _():
                        pair_copy(g, 0, half).start()

                    @pl.when(jnp.logical_and(b == 1, jnp.logical_and(g == 0, k > 0)))
                    def _():
                        hub_sum(1)

                    @pl.when(jnp.logical_and(b == 3, jnp.logical_and(g == 0, k > 0)))
                    def _():
                        hub_finish(1, k - 1, k > 0)

                    @pl.when(jnp.logical_and(b == 1, g == 1))
                    def _():
                        auth_sum(0)

                    @pl.when(jnp.logical_and(b == 3, g == 1))
                    def _():
                        auth_finish(0)

                    @pl.when(o == 1)
                    def _():
                        pair_copy(g, 0, half).wait_recv()
                        part[g, 1, half] = part[g, 1, half] + pair_recv[g, 0, half]
                        x_copy(g, half).start()

                    @pl.when(o == 2)
                    def _():
                        pair_copy(g, 1, half).start()

                    return carry

                return lax.fori_loop(0, 8, chunk, carry)

            lax.fori_loop(0, GROUPS, first_product, 0)

            def second_product(g, carry):
                def row_half(half, carry):
                    for kp in range(4):
                        t = base + 16 + g * 8 + half * 4 + kp
                        if kp == 1:
                            @pl.when(half == 0)
                            def _():
                                auth_pair(g).wait_recv()
                                auth_x(g).wait_recv()
                                auth_forward(g).start()
                        if kp == 3:
                            @pl.when(half == 0)
                            def _():
                                auth_forward(g).wait_recv()
                        block_copy(t, False).wait()
                        lhs = auth[g, :, (own_cols, pair_cols, far_cols, far_pair_cols)[kp]]
                        acc = dot_plain(lhs, ring[t % RING])
                        if kp:
                            acc = acc + part[g, 0, half]
                        part[g, 0, half] = acc
                        block_start(t + RING)
                    y_copy(g, half).start()

                    @pl.when(jnp.logical_and(half == 0, g == 1))
                    def _():
                        hub_sum(0)

                    @pl.when(jnp.logical_and(half == 1, g == 1))
                    def _():
                        hub_finish(0, k, k < sweeps - 1)

                    @pl.when(jnp.logical_and(half == 1, g == 0))
                    def _():
                        auth_sum(1)

                    return carry

                lax.fori_loop(0, 2, row_half, 0)

                def own_step(q, carry):
                    rows = pl.ds(pl.multiple_of(q * step_len, step_len), step_len)
                    cols = pl.ds(pl.multiple_of((q % steps_half) * step_len, step_len), step_len)
                    part[g, 3, q // steps_half, :, cols] = dot_trans(auth[g], res[rows, :])

                    @pl.when(jnp.logical_and(q == 1, g == 0))
                    def _():
                        auth_finish(1)

                    return carry

                return lax.fori_loop(0, n_steps, own_step, carry)

            lax.fori_loop(0, GROUPS, second_product, 0)
            return carry

        lax.fori_loop(0, sweeps, sweep, 0)
        hub_sum(1)
        hub_finish(1, sweeps - 1, None)

    return kernel


def solution(mesh):
    col_size = mesh.shape["col"]
    row_size = mesh.shape["row"]

    def device_fn(adj_tile, pers_piece, restart_wt):
        rows, n_cols = adj_tile.shape
        n_total = rows * row_size
        piece, width = pers_piece.shape
        sweeps = restart_wt.shape[0]
        m = width // GROUPS
        half_len = piece // 2
        far = 1 - lax.axis_index("col")
        adj_t = lax.dynamic_slice(adj_tile, (far * piece, 0), (piece, n_cols)).T
        start = pers_piece.T.reshape(GROUPS, m, piece)
        weights = restart_wt.reshape(sweeps, GROUPS, m).transpose(1, 0, 2)
        weights = jnp.pad(weights, ((0, 0), (0, 0), (0, 128 - m)))
        vmem = pl.BlockSpec(memory_space=pltpu.VMEM)
        hbm = pl.BlockSpec(memory_space=pl.ANY)
        dma = pltpu.SemaphoreType.DMA
        auth_t, hub_t = pl.pallas_call(
            make_kernel(sweeps, n_total, piece, half_len, m),
            out_shape=[jax.ShapeDtypeStruct((GROUPS, m, piece), F32)] * 2,
            in_specs=[hbm, hbm, vmem, vmem],
            out_specs=[vmem, vmem],
            scratch_shapes=[
                pltpu.VMEM((piece, n_cols), BF16),
                pltpu.VMEM((RING, piece, half_len), BF16),
                pltpu.VMEM((GROUPS, 4, 2, m, half_len), F32),
                pltpu.VMEM((GROUPS, 2, 2, m, half_len), F32),
                pltpu.VMEM((GROUPS, 2, m, half_len), F32),
                pltpu.VMEM((GROUPS, m, n_cols), BF16),
                pltpu.VMEM((GROUPS, 2, m, piece), BF16),
                pltpu.VMEM((2, GROUPS, 8, 128), F32),
                pltpu.VMEM((2, GROUPS, 7, 8, 128), F32),
                dma,
                dma((RING,)),
                dma((GROUPS, 2, 2)),
                dma((GROUPS, 2, 2)),
                dma((2, GROUPS, 2)),
                dma((2, GROUPS, 2)),
                dma((2, GROUPS, 7)),
                dma((2, GROUPS, 7)),
                dma((GROUPS, 3)),
                dma((GROUPS, 3)),
                dma((GROUPS,)),
                dma((GROUPS,)),
            ],
            compiler_params=pltpu.CompilerParams(collective_id=0, has_side_effects=True, vmem_limit_bytes=67000000),
            name="hits_sweeps",
        )(adj_tile, adj_t, start, weights)
        return auth_t.reshape(width, piece).T, hub_t.reshape(width, piece).T

    return jax.shard_map(device_fn, mesh=mesh, in_specs=(P("row", "col"), P(("row", "col"), None), P(None, None)), out_specs=(P(("col", "row"), None), P(("row", "col"), None)), check_vma=False)
```

time: 6970 us -> 2630 us (0.38)
  waiting for transfers between devices: 3480 us -> 0 us
  Pallas kernels: 0 us -> 2560 us
  matrix products: 1780 us -> 0 us
  blocking collectives: 1420 us -> 0 us
  other arithmetic: 233 us -> 0 us
  local copies, waits for them, and re-layouts: 3.46 us -> 74.6 us
    pallas_call x0 -> x1, Pallas kernels: none -> 2560 us  [device_fn(): pl.pallas_call(make_kernel(sweeps, n_total, piece, half_len, m), out_shap...]
    reduce_scatter x64 -> x0, waiting for transfers between devices: 2160 us -> none  [the longest x32 1230 us: device_fn(): lax.psum_scatter(auth_part, 'row', scatter_dimension=0, tiled=True)]
    dot_general x64 -> x0, matrix products: 1780 us -> none  [the longest x32 945 us: device_fn(): hub_part = jnp.dot(adj_tile, auth_block, preferred_element_type=jnp.float32)]
    psum x64 -> x0, blocking collectives: 1420 us -> none  [col_normalise(): lax.psum(jnp.sum(local_vals * local_vals, axis=0, keepdims=True), ('col',...]
    all_gather x64 -> x0, waiting for transfers between devices: 1320 us -> none  [the longest x32 680 us: device_fn(): lax.all_gather(auth_vec.astype(jnp.bfloat16), 'row', axis=0, tiled=True)]
    convert_element_type x64 -> x0, other arithmetic: 141 us -> none  [the longest x32 72.3 us: device_fn(): hub_vec.astype(jnp.bfloat16)]
    reduce_sum x64 -> x0, other arithmetic: 88.3 us -> none  [col_normalise(): jnp.sum(local_vals * local_vals, axis=0, keepdims=True)]
  transfers between devices with their start and end apart: 128 -> 0, of which waited for: 128 -> 0; matrix products, arithmetic and copies ran while one was open for 0% -> 0% of each run, Pallas kernels for 0% -> 0%
where the time goes in v1:
time: 2630 us
  Pallas kernels  2560 us (97%)
  local copies, waits for them, and re-layouts  74.6 us (3%)
    pallas_call x1, Pallas kernels, device_fn(): pl.pallas_call(make_kernel(sweeps, n_total, piece, half_len, m), out_shap...  2560 us

profile of v1, /device:TPU:0, one launch (start us, length us, event | category | flops | bytes accessed | tf_op | source)
XLA Modules:
  0.0 2631.4 jit_solution(174707304196082179)
XLA Ops:
  0.6 23.0 constant_dynamic-slice_fusion
  23.6 0.0 copy-start
  23.6 0.0 copy-start.1
  23.6 44.6 %copy.14 = bf16[2048,8192]{0,1:T(8,128)(2,1)} copy(bf16[2048,8192]{1,0:T(8,128)(2,1)} %constant_dynamic-slice_fusion) | data formatting | bytes 67108864
  68.2 0.0 copy-done
  68.2 1.3 copy.10
  69.5 0.0 copy-done.1
  69.5 0.1 reshape.17
  69.6 0.6 pad.4.weights
  70.2 2556.2 %hits_sweeps.1 = (f32[2,64,2048]{2,1,0:T(8,128)}, f32[2,64,2048]{2,1,0:T(8,128)}) custom-call(bf16[4096,8192]{1,0:T(8,128)(2,1)} %adj.1, bf16[8192,2048]{1,0:T(8,128)(2,1)} %bitcast.10, f32[2,64,2048]{2,1,0:T(8,128)} %bitcast.11, f32[2,32,128]{2,1,0:T(8,128)} %pad.4.weights), custom_call_target="tpu_custom_call" | custom-call | tf_op jit(solution)/shard_map/hits_sweeps/pallas_call | solution.py:340
  2626.4 2.5 copy.12
  2628.9 2.5 copy.13
  (1 shorter events, 0.0 us)
Async XLA Ops:
  23.6 44.6 %copy-start = (f32[2048,128]{1,0:T(8,128)S(1)}, f32[2048,128]{1,0:T(8,128)}, u32[]{:S(2)}) copy-start(f32[2048,128]{1,0:T(8,128)} %param.4) | copy-start | bytes 3145732
  23.6 45.9 %copy-start.1 = (f32[32,128]{1,0:T(8,128)S(1)}, f32[32,128]{1,0:T(8,128)}, u32[]{:S(2)}) copy-start(f32[32,128]{1,0:T(8,128)} %param.5) | copy-start | bytes 49156

commit v2 on v1

--- a/solution.py
+++ b/solution.py
@@ -9,11 +9,14 @@
 F32 = jnp.float32
 BF16 = jnp.bfloat16
 GROUPS = 2
-RING = 3
+RING = 4
+HOOKS = (-1, 1, 5, 8, -1, 5, 1, 3)
 
 
 def dot_plain(lhs, rhs):
-    return lax.dot_general(lhs, rhs, (((1,), (0,)), ((), ())), preferred_element_type=F32)
+    lhs = jnp.concatenate([lhs, lhs], axis=0)
+    out = lax.dot_general(lhs, rhs, (((1,), (0,)), ((), ())), preferred_element_type=F32)
+    return out[:lhs.shape[0] // 2]
 
 
 def dot_trans(lhs, rhs):
@@ -21,10 +24,11 @@
 
 
 def make_kernel(sweeps, n_total, piece, half_len, m):
-    n_blocks = sweeps * 32
+    n_slots = sweeps * 4
+    n_blocks = n_slots * 8
     step_len = 512
+    steps_half = half_len // step_len
     n_steps = piece // step_len
-    steps_half = half_len // step_len
 
     def kernel(adj, adj_t, start, weights, auth_out, hub_out, res, ring, part, pair_recv, recv, auth, hub, norm_send, norm_recv,
                res_sem, ring_sem, pair_ss, pair_rs, link_ss, link_rs, norm_ss, norm_rs, auth_ss, auth_rs, hub_ss, hub_rs):
@@ -80,12 +84,18 @@
         def hub_y(g):
             return remote(hub.at[g, 0], hub.at[g, 1], hub_ss.at[g], hub_rs.at[g], y_dev)
 
+        def chunk_of(b):
+            late = b // 4
+            o = (1 - late) * (b % 2) + late * (b // 2)
+            half = (1 - late) * (b // 2) + late * (b % 2)
+            cols = (2 * ((x + 1 - o // 2) % 2) + (c + 1 + o) % 2) * piece + half * half_len
+            return o, half, cols
+
         def block_copy(t, first):
             buf = t % RING
             b = t % 8
             if first:
-                o = b // 2
-                cols = (2 * ((x + 1 - o // 2) % 2) + (c + 1 + o) % 2) * piece + (b % 2) * half_len
+                _, _, cols = chunk_of(b)
                 src = adj.at[pl.ds(far_row, piece), pl.ds(pl.multiple_of(cols, half_len), half_len)]
             else:
                 kp = b % 4
@@ -95,7 +105,9 @@
             return pltpu.make_async_copy(src, ring.at[buf], ring_sem.at[buf])
 
         def block_start(t):
-            first = (t // 8) % 4 < 2
+            u = t // 8
+            place = (u + 1) % 4
+            first = jnp.logical_and(jnp.logical_or(jnp.logical_or(place == 0, place == 3), u == 0), u < n_slots - 1)
 
             @pl.when(jnp.logical_and(t < n_blocks, first))
             def _():
@@ -201,117 +213,129 @@
             hub_y(g).start()
         res_copy.wait()
 
+        def first_product(g, u, hooks):
+            for at, cond, fn in hooks:
+                if at < 0:
+                    pl.when(cond)(fn)
+
+            def chunk(b, carry):
+                t = u * 8 + b
+                o, half, cols = chunk_of(b)
+
+                part[g, o, half] = dot_plain(hub[g, 0], res[:, pl.ds(pl.multiple_of(cols, half_len), half_len)])
+
+                @pl.when(b == 0)
+                def _():
+                    hub_y(g).wait()
+
+                block_copy(t, True).wait()
+                part[g, o, half] = part[g, o, half] + dot_plain(hub[g, 1], ring[t % RING])
+                block_start(t + RING)
+
+                @pl.when(o == 0)
+                def _():
+                    pair_copy(g, 0, half).start()
+
+                for at, cond, fn in hooks:
+                    if at >= 0:
+                        pl.when(jnp.logical_and(b == at, cond))(fn)
+
+                @pl.when(o == 1)
+                def _():
+                    pair_copy(g, 0, half).wait_recv()
+                    part[g, 1, half] = part[g, 1, half] + pair_recv[g, 0, half]
+                    x_copy(g, half).start()
+
+                @pl.when(o == 2)
+                def _():
+                    pair_copy(g, 1, half).start()
+
+                return carry
+
+            lax.fori_loop(0, 8, chunk, 0)
+
+        def second_product(g, u, hooks):
+            for at, cond, fn in hooks:
+                if at < 0:
+                    pl.when(cond)(fn)
+
+            def row_half(half, carry):
+                for kp in range(4):
+                    t = u * 8 + half * 4 + kp
+                    if kp == 1:
+                        @pl.when(half == 0)
+                        def _():
+                            auth_pair(g).wait_recv()
+                    if kp == 2:
+                        @pl.when(half == 0)
+                        def _():
+                            auth_x(g).wait_recv()
+                            auth_forward(g).start()
+                    if kp == 3:
+                        @pl.when(half == 0)
+                        def _():
+                            auth_forward(g).wait_recv()
+                    block_copy(t, False).wait()
+                    lhs_base = (2 * ((x + kp // 2) % 2) + (c + kp) % 2) * piece
+
+                    acc = dot_plain(auth[g, :, pl.ds(pl.multiple_of(lhs_base, piece), piece)], ring[t % RING])
+                    if kp:
+                        acc = acc + part[g, 0, half]
+                    part[g, 0, half] = acc
+                    block_start(t + RING)
+                    for at, cond, fn in hooks:
+                        if 0 <= at < 8 and at % 4 == kp:
+                            pl.when(jnp.logical_and(half == at // 4, cond))(fn)
+                y_copy(g, half).start()
+                return carry
+
+            lax.fori_loop(0, 2, row_half, 0)
+
+            def own_step(q, carry):
+                row = pl.multiple_of(q * step_len, step_len)
+
+                cols = pl.ds(pl.multiple_of((q % steps_half) * step_len, step_len), step_len)
+                part[g, 3, q // steps_half, :, cols] = dot_trans(auth[g], res[pl.ds(row, step_len), :])
+                for at, cond, fn in hooks:
+                    if at >= 8:
+                        pl.when(jnp.logical_and(q == at - 8, cond))(fn)
+                return carry
+
+            lax.fori_loop(0, n_steps, own_step, 0)
+
         def sweep(k, carry):
-            base = k * 32
-
-            def first_product(g, carry):
-                def chunk(b, carry):
-                    t = base + g * 8 + b
-                    o, half = b // 2, b % 2
-                    cols = (2 * ((x + 1 - o // 2) % 2) + (c + 1 + o) % 2) * piece + half * half_len
-
-                    @pl.when(b == 0)
-                    def _():
-                        hub_y(g).wait()
-
-                    block_copy(t, True).wait()
-                    acc = dot_plain(hub[g, 1], ring[t % RING])
-                    acc = acc + dot_plain(hub[g, 0], res[:, pl.ds(pl.multiple_of(cols, half_len), half_len)])
-                    part[g, o, half] = acc
-                    block_start(t + RING)
-
-                    @pl.when(o == 0)
-                    def _():
-                        pair_copy(g, 0, half).start()
-
-                    @pl.when(jnp.logical_and(b == 1, jnp.logical_and(g == 0, k > 0)))
-                    def _():
-                        hub_sum(1)
-
-                    @pl.when(jnp.logical_and(b == 3, jnp.logical_and(g == 0, k > 0)))
-                    def _():
-                        hub_finish(1, k - 1, k > 0)
-
-                    @pl.when(jnp.logical_and(b == 1, g == 1))
-                    def _():
-                        auth_sum(0)
-
-                    @pl.when(jnp.logical_and(b == 3, g == 1))
-                    def _():
-                        auth_finish(0)
-
-                    @pl.when(o == 1)
-                    def _():
-                        pair_copy(g, 0, half).wait_recv()
-                        part[g, 1, half] = part[g, 1, half] + pair_recv[g, 0, half]
-                        x_copy(g, half).start()
-
-                    @pl.when(o == 2)
-                    def _():
-                        pair_copy(g, 1, half).start()
-
-                    return carry
-
-                return lax.fori_loop(0, 8, chunk, carry)
-
-            lax.fori_loop(0, GROUPS, first_product, 0)
-
-            def second_product(g, carry):
-                def row_half(half, carry):
-                    for kp in range(4):
-                        t = base + 16 + g * 8 + half * 4 + kp
-                        if kp == 1:
-                            @pl.when(half == 0)
-                            def _():
-                                auth_pair(g).wait_recv()
-                                auth_x(g).wait_recv()
-                                auth_forward(g).start()
-                        if kp == 3:
-                            @pl.when(half == 0)
-                            def _():
-                                auth_forward(g).wait_recv()
-                        block_copy(t, False).wait()
-                        lhs = auth[g, :, (own_cols, pair_cols, far_cols, far_pair_cols)[kp]]
-                        acc = dot_plain(lhs, ring[t % RING])
-                        if kp:
-                            acc = acc + part[g, 0, half]
-                        part[g, 0, half] = acc
-                        block_start(t + RING)
-                    y_copy(g, half).start()
-
-                    @pl.when(jnp.logical_and(half == 0, g == 1))
-                    def _():
-                        hub_sum(0)
-
-                    @pl.when(jnp.logical_and(half == 1, g == 1))
-                    def _():
-                        hub_finish(0, k, k < sweeps - 1)
-
-                    @pl.when(jnp.logical_and(half == 1, g == 0))
-                    def _():
-                        auth_sum(1)
-
-                    return carry
-
-                lax.fori_loop(0, 2, row_half, 0)
-
-                def own_step(q, carry):
-                    rows = pl.ds(pl.multiple_of(q * step_len, step_len), step_len)
-                    cols = pl.ds(pl.multiple_of((q % steps_half) * step_len, step_len), step_len)
-                    part[g, 3, q // steps_half, :, cols] = dot_trans(auth[g], res[rows, :])
-
-                    @pl.when(jnp.logical_and(q == 1, g == 0))
-                    def _():
-                        auth_finish(1)
-
-                    return carry
-
-                return lax.fori_loop(0, n_steps, own_step, carry)
-
-            lax.fori_loop(0, GROUPS, second_product, 0)
+            some, more = k > 0, k < sweeps
+
+            @pl.when(more)
+            def _():
+                hooks = [(HOOKS[0], some, lambda: auth_sum(1)), (HOOKS[1], some, lambda: auth_finish(1))]
+                first_product(0, 4 * k - 1 + 1 // (k + 1), hooks)
+
+            @pl.when(jnp.logical_not(more))
+            def _():
+                auth_sum(1)
+                auth_finish(1)
+
+            @pl.when(jnp.logical_not(some))
+            def _():
+                auth_sum(0)
+                auth_finish(0)
+
+            @pl.when(some)
+            def _():
+                hooks = [(HOOKS[2], more, lambda: auth_sum(0)), (HOOKS[3], more, lambda: auth_finish(0))]
+                second_product(1, 4 * k - k // sweeps, hooks)
+
+            @pl.when(more)
+            def _():
+                hooks = [(HOOKS[4], some, lambda: hub_sum(1)), (HOOKS[5], some, lambda: hub_finish(1, k - 1, some))]
+                second_product(0, 4 * k + 1, hooks)
+                hooks = [(HOOKS[6], more, lambda: hub_sum(0)), (HOOKS[7], more, lambda: hub_finish(0, k, k < sweeps - 1))]
+                first_product(1, 4 * k + 2, hooks)
+
             return carry
 
-        lax.fori_loop(0, sweeps, sweep, 0)
+        lax.fori_loop(0, sweeps + 1, sweep, 0)
         hub_sum(1)
         hub_finish(1, sweeps - 1, None)
 

time: 2630 us -> 2380 us (0.905)
  Pallas kernels: 2560 us -> 2310 us
    pallas_call x1, Pallas kernels: 2560 us -> 2310 us  [device_fn(): pl.pallas_call(make_kernel(sweeps, n_total, piece, half_len, m), out_shap...]
where the time goes in v2:
time: 2380 us
  Pallas kernels  2310 us (97%)
  local copies, waits for them, and re-layouts  74.6 us (3%)
    pallas_call x1, Pallas kernels, device_fn(): pl.pallas_call(make_kernel(sweeps, n_total, piece, half_len, m), out_shap...  2310 us

profile of v2, /device:TPU:0, one launch (start us, length us, event | category | flops | bytes accessed | tf_op | source)
XLA Modules:
  0.0 2382.2 jit_solution(8932372628243307246)
XLA Ops:
  0.6 23.0 constant_dynamic-slice_fusion
  23.6 0.0 copy-start
  23.6 0.0 copy-start.1
  23.6 44.6 %copy.14 = bf16[2048,8192]{0,1:T(8,128)(2,1)} copy(bf16[2048,8192]{1,0:T(8,128)(2,1)} %constant_dynamic-slice_fusion) | data formatting | bytes 67108864
  68.2 0.0 copy-done
  68.2 1.3 copy.10
  69.5 0.0 copy-done.1
  69.5 0.1 reshape.17
  69.6 0.6 pad.4.weights
  70.2 2306.9 %hits_sweeps.1 = (f32[2,64,2048]{2,1,0:T(8,128)}, f32[2,64,2048]{2,1,0:T(8,128)}) custom-call(bf16[4096,8192]{1,0:T(8,128)(2,1)} %adj.1, bf16[8192,2048]{1,0:T(8,128)(2,1)} %bitcast.10, f32[2,64,2048]{2,1,0:T(8,128)} %bitcast.11, f32[2,32,128]{2,1,0:T(8,128)} %pad.4.weights), custom_call_target="tpu_custom_call" | custom-call | tf_op jit(solution)/shard_map/hits_sweeps/pallas_call | solution.py:364
  2377.1 2.5 copy.12
  2379.6 2.5 copy.13
  (1 shorter events, 0.0 us)
Async XLA Ops:
  23.6 44.6 %copy-start = (f32[2048,128]{1,0:T(8,128)S(1)}, f32[2048,128]{1,0:T(8,128)}, u32[]{:S(2)}) copy-start(f32[2048,128]{1,0:T(8,128)} %param.4) | copy-start | bytes 3145732
  23.6 45.9 %copy-start.1 = (f32[32,128]{1,0:T(8,128)S(1)}, f32[32,128]{1,0:T(8,128)}, u32[]{:S(2)}) copy-start(f32[32,128]{1,0:T(8,128)} %param.5) | copy-start | bytes 49156
